TPU v7x, 512 devices: a whole 4x4x16 slice. The times are simulated.
512 devices in a mesh: learner: 16 (over y, x), rollout: 8 (over z_lo), dp: 4 (over z_hi, core).
Axes of the slice: x: 4, y: 4, z: 16 (z_hi: 2, z_lo: 8; z = z_hi * 8 + z_lo), core: 2. Of those that a mesh axis runs over, the one named last changes fastest.
Arguments:
- weight_delta: float32 [8192, 14336], P(('rollout', 'dp'), 'learner'), may hold values from -0.48 to 0.48
- sketch_seed: int32 [1], replicated, may hold values from 0 to 1048575
- up_weight: bfloat16 [8192, 14336], P('rollout', 'learner'), may hold values from -0.0625 to 0.0625
- down_weight: bfloat16 [14336, 8192], P('learner', 'rollout'), may hold values from -0.046875 to 0.046875
- norm_gain: bfloat16 [8192], P('rollout'), may hold values from 0.5 to 1.5
- state_pool: bfloat16 [128, 8192], P(None, 'rollout'), may hold values from -12 to 12
- token_rows: int32 [2, 4, 128], P(None, 'dp'), may hold values from 0 to 127
Outputs:
- decoded: bfloat16 [4, 128, 8192], P('dp', 'learner', 'rollout')
All inputs are finite; a program needn't handle non-finite values.
Results may differ from a plain program's by a relative error of at most 0.017.
Values may be sent and summed in bfloat16 or wider, within the bound.
No kernel may reach another device: no remote copies, remote signals or barrier semaphores. Data moves between devices by JAX's collectives and lax.ppermute only.
A program may use at most 64 MiB of HBM per device.

v0:
```python
import functools

import jax
import jax.numpy as jnp
from jax import lax
from jax.experimental import pallas as pl
from jax.experimental.pallas import tpu as pltpu
from jax.sharding import Mesh
from jax.sharding import PartitionSpec as P


D = 8192
RANK = 128
EPS = 1e-05
L = ("y", "x")
CL = ("c", "y", "x")
Z = ("zl", "zh")
BF = jnp.bfloat16
F32 = jnp.float32


def swap(x, axis):
    return lax.all_to_all(x, axis, split_axis=0, concat_axis=0, tiled=True)


def dot(a, b):
    return jnp.dot(a, b, preferred_element_type=F32)


def dot_t(a, b):
    return lax.dot_general(a, b, (((0,), (0,)), ((), ())), preferred_element_type=F32)


def hi_lo(x):
    hi = x.astype(BF).astype(F32)
    return hi, x - hi


def diagonal_offset(rows, first):
    row = first + lax.broadcasted_iota(jnp.int32, (rows, RANK), 0)
    col = lax.broadcasted_iota(jnp.int32, (rows, RANK), 1)
    return (col - row) & (RANK - 1)


def packed(gram, squares, offset):
    hi, lo = hi_lo(squares)
    rest = jnp.where(offset == RANK - 1, lo, jnp.where(offset == RANK - 2, hi, 0.0))
    return jnp.where(offset <= RANK // 2, gram, rest)


def unpacked_squares(gram, offset):
    return jnp.sum(jnp.where(offset >= RANK - 2, gram, 0.0), axis=1, keepdims=True)


def precise(a, b):
    return jnp.dot(a, b, precision=lax.Precision.HIGHEST, preferred_element_type=F32)


def silu(x):
    return x / (1.0 + jnp.exp(-x))


def total(ref):
    return jnp.sum(ref[...].astype(F32), axis=0)


HBM = pl.BlockSpec(memory_space=pltpu.HBM)
VMEM = pl.BlockSpec(memory_space=pltpu.VMEM)


def call(kernel, shapes, place, *arrays, hbm=None, scratch=(), limit=16):
    specs = [pl.BlockSpec(memory_space=pltpu.SMEM)]
    if hbm is not None:
        arrays = (hbm, *arrays)
        specs += [HBM]
        scratch = (*scratch, pltpu.SemaphoreType.DMA((2,)))
    specs += [VMEM] * (len(arrays) - (hbm is not None))
    return pl.pallas_call(
        kernel,
        out_shape=tuple(jax.ShapeDtypeStruct(shape, BF) for shape in shapes),
        in_specs=specs,
        out_specs=(VMEM,) * len(shapes),
        scratch_shapes=scratch,
        compiler_params=pltpu.CompilerParams(vmem_limit_bytes=int(limit * 1024 * 1024)),
    )(place, *arrays)


def column(row):
    return jnp.broadcast_to(row, (RANK, RANK)).T


def chosen(tokens, step):
    count = tokens.shape[0] // 2
    rows = tokens[step * count : (step + 1) * count].astype(F32)
    lane = lax.broadcasted_iota(jnp.int32, (count, RANK), 1).astype(F32)
    return jnp.where(rows == lane, 1.0, 0.0).astype(BF)


def picks(place, kept_ref, got_ref, step):
    half = kept_ref.shape[1] - RANK // 2
    mine = chosen(kept_ref[:, half : half + 1], step)
    theirs = chosen(got_ref[:, half : half + 1], step)
    first = place[0] == 0
    return jnp.concatenate(
        [jnp.where(first, mine, theirs), jnp.where(first, theirs, mine)], axis=0
    )


def own_half(place, x):
    half = x.shape[1] // 2
    return jnp.where(place[0] == 0, x[:, :half], x[:, half:])


def range_kernel(place, delta_hbm, part_ref, delta_ref, sem):
    rows, cols = delta_ref.shape
    split = rows // 2
    copies = [
        pltpu.make_async_copy(
            delta_hbm.at[pl.ds(i * split, split)], delta_ref.at[pl.ds(i * split, split)], sem.at[i]
        )
        for i in range(2)
    ]
    for copy in copies:
        copy.start()
    row_index = place[3] + lax.broadcasted_iota(jnp.int32, (cols, RANK), 0)
    col_index = lax.broadcasted_iota(jnp.int32, (cols, RANK), 1)
    hashed = row_index * RANK + col_index + place[4]
    hashed = hashed * 1103515245 + 12345
    hashed = hashed ^ lax.shift_right_logical(hashed, jnp.int32(16))
    hashed = hashed * 73244475
    hashed = hashed ^ lax.shift_right_logical(hashed, jnp.int32(15))
    parity = lax.shift_right_logical(hashed, jnp.int32(11)) & 1
    signs = (2 * parity - 1).astype(F32).astype(BF)
    for i, copy in enumerate(copies):
        copy.wait()
        span = slice(i * split, (i + 1) * split)
        delta = delta_ref[span].astype(BF)
        parts = part_ref.shape[0] // 2
        part_ref[i * parts : (i + 1) * parts] = (
            dot(delta, signs).astype(BF).reshape(parts, *part_ref.shape[1:])
        )


def halves_kernel(place, delta_ref, tokens_ref, kept_ref, sent_ref):
    core = place[0]
    half = delta_ref.shape[1] // 2
    delta = delta_ref[...].astype(BF)
    left, right = delta[:, :half], delta[:, half:]
    tokens = jnp.concatenate([column(tokens_ref[i : i + 1].astype(F32)) for i in range(2)], axis=0)
    tokens = tokens[:, : RANK // 2].astype(BF)
    kept_ref[...] = jnp.concatenate([jnp.where(core == 0, left, right), tokens], axis=1)
    sent_ref[...] = jnp.concatenate([jnp.where(core == 0, right, left), tokens], axis=1)


def pick_kernel(place, kept_ref, got_ref, pick_ref):
    for step in range(2):
        pick_ref[step] = picks(place, kept_ref, got_ref, step)


def pool_kernel(place, up_hbm, pool_ref, gain_ref, gained_ref, up_out_ref, squares_ref, up_ref, sem):
    z_half = place[1]
    width = up_ref.shape[0]
    first = pl.multiple_of(z_half * width, width)
    copy = pltpu.make_async_copy(up_hbm.at[pl.ds(first, width)], up_ref, sem.at[0])
    copy.start()
    pool = jnp.where(z_half == 0, pool_ref[:, :width], pool_ref[:, width:]).astype(F32)
    gain = jnp.where(z_half == 0, gain_ref[:, :width], gain_ref[:, width:])
    gained = (pool * gain).astype(BF)
    gained_ref[...] = gained
    squares = jnp.broadcast_to(jnp.sum(pool * pool, axis=1, keepdims=True), (pool.shape[0], RANK))
    hi, lo = hi_lo(squares)
    squares_ref[0] = hi.astype(BF)
    squares_ref[1] = lo.astype(BF)
    copy.wait()
    up_out_ref[...] = own_half(place, dot(gained, up_ref[...])).astype(BF)


def spread_kernel(place, parts_ref, out_ref):
    out_ref[...] = jnp.broadcast_to(total(parts_ref).astype(BF), out_ref.shape)


def moved_kernel(place, basis_ref, kept_ref, got_ref, pool_ref, up_ref, squares_ref, out_ref):
    core = place[0]
    rows, wide = kept_ref.shape
    half = wide - RANK // 2
    count = basis_ref.shape[0] // 2
    own = basis_ref[pl.ds(core * count, count)].reshape(rows, RANK)
    other = basis_ref[pl.ds((1 - core) * count, count)].reshape(rows, RANK)
    basis = basis_ref[...].reshape(2 * rows, RANK)

    def put(first, values):
        values = values.astype(BF)
        out_ref[:, :, first : first + values.shape[1]] = values.reshape(
            *out_ref.shape[:2], values.shape[1]
        )

    moved = dot_t(own, kept_ref[...]) + dot_t(other, got_ref[...])
    put(0, jnp.concatenate([moved[:, :half].astype(BF), up_ref[...]], axis=1))
    squares = squares_ref[0].astype(F32) + squares_ref[1].astype(F32)
    put(2 * half, packed(dot_t(basis, basis), squares, diagonal_offset(RANK, 0)))
    put(2 * half + RANK, dot(pool_ref[...], basis))


def share_kernel(place, parts_ref, out_ref):
    share = total(parts_ref)
    rows, width = share.shape
    first = width - 2 * RANK
    offset = diagonal_offset(rows, place[2] * rows)
    gram = share[:, first : first + RANK]
    gram = packed(gram, unpacked_squares(gram, offset), offset)
    share = jnp.concatenate([share[:, :first], gram, share[:, first + RANK :]], axis=1)
    out_ref[...] = jnp.broadcast_to(share.astype(BF), out_ref.shape)


def down_copy(place, down_hbm, down_ref, sem):
    half = down_ref.shape[0]
    first = pl.multiple_of(place[0] * half, RANK // 2)
    return pltpu.make_async_copy(down_hbm.at[pl.ds(first, half)], down_ref, sem.at[0])


def first_kernel(place, down_hbm, z_ref, step_ref, coef_ref, pre_ref, down_ref, sem):
    copy = down_copy(place, down_hbm, down_ref, sem)
    copy.start()
    half = coef_ref.shape[1]
    gathered = z_ref[...].reshape(RANK, z_ref.shape[2])
    gram = gathered[:, 2 * half : 2 * half + RANK].astype(F32)
    row = lax.broadcasted_iota(jnp.int32, (RANK, RANK), 0)
    col = lax.broadcasted_iota(jnp.int32, (RANK, RANK), 1)
    offset = (col - row) & (RANK - 1)
    squares = unpacked_squares(gram, offset)
    gram = jnp.where(offset <= RANK // 2, gram, gram.T)
    eye = jnp.where(row == col, 1.0, 0.0)
    on_diag = gram * eye
    scale_col = lax.rsqrt(jnp.sum(on_diag, axis=1, keepdims=True))
    scale_row = lax.rsqrt(jnp.sum(on_diag, axis=0, keepdims=True))
    unit = gram * scale_col * scale_row
    bound = jnp.max(jnp.sum(jnp.abs(unit), axis=1, keepdims=True), axis=0, keepdims=True)
    step = 2.0 / (1.0 + bound)
    start = step * (2.0 * eye - step * unit)

    def going(state):
        count, error, _ = state
        return jnp.logical_and(count < 40, error > 2e-4)

    def refine(state):
        count, _, inverse = state
        left = eye - precise(unit, inverse)
        moved = dot(inverse.astype(BF), left.astype(BF))
        return count + 1, jnp.sum(left * left), inverse + moved

    _, _, inverse = lax.while_loop(going, refine, (0, jnp.float32(1.0), start))
    hi, lo = hi_lo(inverse * scale_col * scale_row)
    moved = gathered[:, :half]
    coef = (dot(hi.astype(BF), moved) + dot(lo.astype(BF), moved)).astype(BF)
    coef_ref[...] = coef
    pre = gathered[:, half : 2 * half].astype(F32) + dot(gathered[:, 2 * half + RANK :], coef)
    pre_ref[...] = pre.astype(BF)
    hidden = silu(pre * lax.rsqrt(squares / D + EPS)).astype(BF)
    copy.wait()
    result = dot(hidden, down_ref[...]).astype(BF)
    count, rows, width = step_ref.shape
    step_ref[: count // 2] = result[:, :width].reshape(count // 2, rows, width)
    step_ref[count // 2 :] = result[:, width:].reshape(count // 2, rows, width)


def second_kernel(
    place, up_hbm, step_ref, pool_ref, gain_ref, basis_ref, coef_ref, pick_ref, out_ref, rows_ref, up_ref, sem
):
    z_half = place[1]
    _, _, width = step_ref.shape
    pool_rows = pool_ref.shape[0]
    start = pl.multiple_of(z_half * width, width)
    copy = pltpu.make_async_copy(up_hbm.at[pl.ds(start, width)], up_ref, sem.at[0])
    copy.start()
    half = coef_ref.shape[1]
    basis = basis_ref[...].reshape(width, RANK)
    step = step_ref[...].astype(F32).reshape(2, pool_rows, width)
    pool = pool_ref[...]
    left = (pool[:, :width].astype(F32) + step[0]).astype(BF)
    right = (pool[:, width:].astype(F32) + step[1]).astype(BF)
    carried = jnp.concatenate([left, right], axis=1)
    gain = jnp.where(z_half == 0, gain_ref[:, :width], gain_ref[:, width:])
    gained = (jnp.where(z_half == 0, left, right).astype(F32) * gain).astype(BF)

    def second(one, two):
        return (dot(one, carried) + dot(two, pool)).astype(BF)

    wide = second(pick_ref[0], pick_ref[1]).astype(F32)
    squares = jnp.sum(wide * wide, axis=1, keepdims=True)
    row = lax.broadcasted_iota(jnp.int32, (rows_ref.shape[0], pool_rows), 0)
    lane = lax.broadcasted_iota(jnp.int32, (rows_ref.shape[0], pool_rows), 1)
    here = jnp.where(lane == row + place[5], 1.0, 0.0).astype(BF)
    own = [
        dot(here, jnp.where(place[0] == 0, pick_ref[i, :pool_rows], pick_ref[i, pool_rows:]))
        for i in range(2)
    ]
    rows_ref[...] = second(own[0].astype(BF), own[1].astype(BF))
    lane = lax.broadcasted_iota(jnp.int32, (pool_rows, out_ref.shape[2] - half), 1)
    first = 4 * z_half
    tail = jnp.zeros(lane.shape, F32)
    for place_in, value in enumerate((*hi_lo(squares[:pool_rows]), *hi_lo(squares[pool_rows:]))):
        tail = jnp.where(lane == first + place_in, value, tail)
    low = dot(dot(gained, basis).astype(BF), coef_ref[...])
    copy.wait()
    up = own_half(place, dot(gained, up_ref[...])) + low
    both = jnp.concatenate([up.astype(BF), tail.astype(BF)], axis=1)
    out_ref[...] = both.reshape(out_ref.shape)


def second_share_kernel(half, place, parts_ref, out_ref):
    share = total(parts_ref)
    lane = lax.broadcasted_iota(jnp.int32, share.shape, 1)
    out = share
    for first in range(half, half + 8, 2):
        whole = jnp.where(jnp.logical_or(lane == first, lane == first + 1), share, 0.0)
        hi, lo = hi_lo(jnp.sum(whole, axis=1, keepdims=True))
        out = jnp.where(lane == first, hi, jnp.where(lane == first + 1, lo, out))
    out_ref[...] = jnp.broadcast_to(out.astype(BF), out_ref.shape)


def last_kernel(place, down_hbm, z_ref, pre_ref, pick_ref, out_ref, down_ref, sem):
    copy = down_copy(place, down_hbm, down_ref, sem)
    copy.start()
    z_half = place[1]
    half = pre_ref.shape[1]
    pool_rows = pre_ref.shape[0]
    gathered = z_ref[...].reshape(pool_rows, z_ref.shape[2])
    lane = lax.broadcasted_iota(jnp.int32, gathered.shape, 1)

    def squares(first):
        first = half + 4 * z_half + first
        chosen = jnp.logical_or(lane == first, lane == first + 1)
        return jnp.sum(jnp.where(chosen, gathered.astype(F32), 0.0), axis=1, keepdims=True)

    scale = lax.rsqrt(jnp.concatenate([squares(0), squares(2)], axis=0) / D + EPS)
    pre = dot(pick_ref[0], gathered[:, :half]) + dot(pick_ref[1], pre_ref[...])
    hidden = silu(pre * scale).astype(BF)
    copy.wait()
    out_ref[...] = dot(hidden, down_ref[...]).astype(BF).reshape(out_ref.shape)


def staged(weight_delta, sketch_seed, up_weight, down_weight, norm_gain, state_pool, token_rows):
    learner = lax.axis_index(L)
    rows, cols = weight_delta.shape
    half = cols // 2
    width = 2 * rows
    count = state_pool.shape[0]
    out_rows = count // 16
    place = jnp.stack(
        [
            lax.axis_index("c"),
            lax.axis_index("zh"),
            lax.axis_index(Z),
            learner * cols,
            sketch_seed[0] * 7919,
            learner * out_rows,
        ]
    ).astype(jnp.int32)
    padded = half + RANK // 2
    (part,) = call(
        range_kernel,
        ((16, rows // 16, RANK),),
        place,
        hbm=weight_delta,
        scratch=(pltpu.VMEM((rows, cols), F32),),
        limit=63.5,
    )
    kept, sent = call(
        halves_kernel, ((rows, padded), (rows, padded)), place, weight_delta, token_rows[:, 0, :]
    )
    received = lax.ppermute(sent, "c", [(0, 1), (1, 0)])
    parts = swap(part, L)
    gain = norm_gain.astype(F32)[None]
    up_scratch = (pltpu.VMEM((width, cols), BF),)
    down_scratch = (pltpu.VMEM((half, 2 * width), BF),)
    parts, place, gain, pool = lax.optimization_barrier((parts, place, gain, state_pool))
    (spread,) = call(spread_kernel, ((32, rows // 16, RANK),), place, parts)
    basis = swap(spread, CL)
    (pick,) = call(pick_kernel, ((2, 2 * count, count),), place, kept, received)
    gained, pool_up, squares = call(
        pool_kernel,
        ((count, width), (count, half), (2, count, RANK)),
        place, pool, gain,
        hbm=up_weight, scratch=up_scratch,
    )
    (stacked,) = call(
        moved_kernel,
        ((16, count // 16, 2 * half + 2 * RANK),),
        place, basis, kept, received, gained, pool_up, squares,
    )
    (share,) = call(share_kernel, (stacked.shape,), place, swap(stacked, Z))
    step_part, coef, pool_pre = call(
        first_kernel,
        ((32, count // 16, width), (RANK, half), (count, half)),
        place, swap(share, Z),
        hbm=down_weight, scratch=down_scratch,
    )
    (spread,) = call(spread_kernel, (step_part.shape,), place, swap(step_part, CL))
    step = swap(spread, CL)
    stacked, own_second = call(
        second_kernel,
        ((16, count // 16, padded), (out_rows, 2 * width)),
        place, step, pool, gain, basis, coef, pick,
        hbm=up_weight, scratch=up_scratch,
    )
    (share,) = call(
        functools.partial(second_share_kernel, half), (stacked.shape,), place, swap(stacked, Z)
    )
    (last,) = call(
        last_kernel,
        ((32, out_rows, 2 * width),),
        place, swap(share, Z), pool_pre, pick,
        hbm=down_weight, scratch=down_scratch,
    )
    last_share = jnp.sum(swap(last, CL).astype(F32), axis=0)
    return (own_second.astype(F32) + last_share).astype(BF)[None]


def solution(mesh):
    torus = Mesh(
        mesh.devices.reshape(4, 4, mesh.shape["rollout"], 2, 2), ("y", "x", "zl", "zh", "c")
    )
    return jax.shard_map(
        staged,
        mesh=torus,
        in_specs=(
            P(("zl", "zh", "c"), L),
            P(),
            P("zl", L),
            P(L, "zl"),
            P("zl"),
            P(None, "zl"),
            P(None, ("zh", "c"), None),
        ),
        out_specs=P(("zh", "c"), L, "zl"),
        check_vma=False,
    )
```

profile of v0, /device:TPU:1, one launch (start us, length us, event | category | flops | bytes accessed | tf_op | source)
XLA Modules:
  0.0 190.9 jit_solution(6221837202830812827)
XLA Ops:
  0.8 1.2 copy-done.4
  1.9 0.7 copy-done.12
  2.6 1.6 shard_map.75
  4.2 0.7 copy-done.6
  4.9 8.7 %collective-permute-start = (bf16[256,512]{1,0:T(8,128)(2,1)}, bf16[256,512]{1,0:T(8,128)(2,1)}, u32[]{:S(2)}, u32[]{:S(2)}) collective-permute-start(bf16[256,512]{1,0:T(8,128)(2,1)} %get-tuple-element.22), channel_id=1, source_target_pairs={{0,1},{1,0},{2,3},{3,2},{4,5},{5,4},{6,7},{7,6},{8,9},{9,8},{10,11... | collective-permute-start | bytes 786440 | tf_op jit(solution)/shard_map/ppermute | solution.py:371
  13.6 2.8 %shard_map.73 = bf16[16,16,128]{2,1,0:T(8,128)(2,1)} custom-call(s32[6]{0:T(128)} %copy-done.8, f32[256,896]{1,0:T(8,128)} %delta_ref.1), custom_call_target="tpu_custom_call" | custom-call | tf_op jit(solution)/shard_map/pallas_call | solution.py:78
  16.4 3.6 %all-to-all-start = ((bf16[16,16,128]{2,1,0:T(8,128)(2,1)}), bf16[16,16,128]{2,1,0:T(8,128)(2,1)S(1)}, u32[]{:S(2)}, u32[]{:S(2)}) async-start(bf16[16,16,128]{2,1,0:T(8,128)(2,1)} %shard_map.73), calls=%async_computation | async-start | bytes 131072 | tf_op jit(solution)/shard_map/all_to_all | solution.py:23
  20.1 6.7 %all-to-all-done.parts_ref = bf16[16,16,128]{2,1,0:T(8,128)(2,1)S(1)} async-done(((bf16[16,16,128]{2,1,0:T(8,128)(2,1)}), bf16[16,16,128]{2,1,0:T(8,128)(2,1)S(1)}, u32[]{:S(2)}, u32[]{:S(2)}) %all-to-all-start) | async-done | bytes 65568 | tf_op jit(solution)/shard_map/all_to_all | solution.py:23
  26.8 0.7 copy-done.9
  27.5 1.2 shard_map.74
  28.7 4.5 %all-to-all-start.1 = ((bf16[32,16,128]{2,1,0:T(8,128)(2,1)}), bf16[32,16,128]{2,1,0:T(8,128)(2,1)S(1)}, u32[]{:S(2)}, u32[]{:S(2)}) async-start(bf16[32,16,128]{2,1,0:T(8,128)(2,1)} %shard_map.74), calls=%async_computation.1 | async-start | bytes 262144 | tf_op jit(solution)/shard_map/all_to_all | solution.py:23
  33.2 1.5 copy-done
  34.7 0.7 copy-done.10
  35.3 1.3 shard_map.76
  36.7 4.1 %all-to-all-done.1.basis_ref = bf16[32,16,128]{2,1,0:T(8,128)(2,1)S(1)} async-done(((bf16[32,16,128]{2,1,0:T(8,128)(2,1)}), bf16[32,16,128]{2,1,0:T(8,128)(2,1)S(1)}, u32[]{:S(2)}, u32[]{:S(2)}) %all-to-all-start.1) | async-done | bytes 131104 | tf_op jit(solution)/shard_map/all_to_all | solution.py:23
  40.7 1.4 shard_map.77
  42.2 30.8 %all_to_all.45.parts_ref = bf16[16,8,1152]{2,1,0:T(8,128)(2,1)S(1)} all-to-all(bf16[16,8,1152]{2,1,0:T(8,128)(2,1)S(1)} %shard_map.77), channel_id=1, replica_groups=mesh['y'=4,'x'=4,'zl'=8,'zh'=2,'c'=2] {'zl','zh'}, dimensions={0} | all-to-all | bytes 589824 | tf_op jit(solution)/shard_map/all_to_all | solution.py:23
  73.0 0.7 shard_map.78
  73.7 23.7 %all_to_all.46.z_ref = bf16[16,8,1152]{2,1,0:T(8,128)(2,1)S(1)} all-to-all(bf16[16,8,1152]{2,1,0:T(8,128)(2,1)S(1)} %shard_map.78), channel_id=1, replica_groups=mesh['y'=4,'x'=4,'zl'=8,'zh'=2,'c'=2] {'zl','zh'}, dimensions={0} | all-to-all | bytes 589824 | tf_op jit(solution)/shard_map/all_to_all | solution.py:23
  97.3 4.3 %shard_map.79 = (bf16[32,8,512]{2,1,0:T(8,128)(2,1)S(1)}, bf16[128,448]{1,0:T(8,128)(2,1)S(1)}, bf16[128,448]{1,0:T(8,128)(2,1)S(1)}) custom-call(s32[6]{0:T(128)S(1)} %copy-done.11, bf16[896,1024]{1,0:T(8,128)(2,1)S(1)} %copy-done.2, bf16[16,8,1152]{2,1,0:T(8,128)(2,1)S(1)} %all_to_all.46.z_ref), custom_call_target="tpu_custom_call" | custom-call | tf_op jit(solution)/shard_map/pallas_call | solution.py:78
  101.7 17.0 %all_to_all.47.parts_ref = bf16[32,8,512]{2,1,0:T(8,128)(2,1)S(1)} all-to-all(bf16[32,8,512]{2,1,0:T(8,128)(2,1)S(1)} %get-tuple-element.28), channel_id=1, replica_groups=mesh['y'=4,'x'=4,'zl'=8,'zh'=2,'c'=2] {'c','y','x'}, dimensions={0} | all-to-all | bytes 524288 | tf_op jit(solution)/shard_map/all_to_all | solution.py:23
  118.7 1.3 shard_map.80
  119.9 4.6 %all-to-all-start.5 = ((bf16[32,8,512]{2,1,0:T(8,128)(2,1)}), bf16[32,8,512]{2,1,0:T(8,128)(2,1)S(1)}, u32[]{:S(2)}, u32[]{:S(2)}) async-start(bf16[32,8,512]{2,1,0:T(8,128)(2,1)} %shard_map.80), calls=%async_computation.5 | async-start | bytes 524288 | tf_op jit(solution)/shard_map/all_to_all | solution.py:23
  124.6 1.1 shard_map.81.pick_ref
  125.7 7.2 %all-to-all-done.5.step_ref = bf16[32,8,512]{2,1,0:T(8,128)(2,1)S(1)} async-done(((bf16[32,8,512]{2,1,0:T(8,128)(2,1)}), bf16[32,8,512]{2,1,0:T(8,128)(2,1)S(1)}, u32[]{:S(2)}, u32[]{:S(2)}) %all-to-all-start.5) | async-done | bytes 262176 | tf_op jit(solution)/shard_map/all_to_all | solution.py:23
  132.9 2.0 %shard_map.82 = (bf16[16,8,512]{2,1,0:T(8,128)(2,1)S(1)}, bf16[8,1024]{1,0:T(8,128)(2,1)S(1)}) custom-call(s32[6]{0:T(128)S(1)} %copy-done.11, bf16[1024,896]{1,0:T(8,128)(2,1)S(1)} %copy-done.1, bf16[32,8,512]{2,1,0:T(8,128)(2,1)S(1)} %all-to-all-done.5.step_ref, bf16[128,1024]{1,0:T(8,128)(2,1)S(1)} %copy-done.5, f32[1,1024]{1,0:T(1,128)S(1)} %bitcast.10, ...), custom_call_target="tpu_custom_call" | custom-call | tf_op jit(solution)/shard_map/pallas_call | solution.py:78
  134.9 17.7 %all_to_all.48.parts_ref = bf16[16,8,512]{2,1,0:T(8,128)(2,1)S(1)} all-to-all(bf16[16,8,512]{2,1,0:T(8,128)(2,1)S(1)} %get-tuple-element.31), channel_id=1, replica_groups=mesh['y'=4,'x'=4,'zl'=8,'zh'=2,'c'=2] {'zl','zh'}, dimensions={0} | all-to-all | bytes 262144 | tf_op jit(solution)/shard_map/all_to_all | solution.py:23
  152.6 0.6 shard_map.83
  153.2 17.6 %all_to_all.49.z_ref = bf16[16,8,512]{2,1,0:T(8,128)(2,1)S(1)} all-to-all(bf16[16,8,512]{2,1,0:T(8,128)(2,1)S(1)} %shard_map.83), channel_id=1, replica_groups=mesh['y'=4,'x'=4,'zl'=8,'zh'=2,'c'=2] {'zl','zh'}, dimensions={0} | all-to-all | bytes 262144 | tf_op jit(solution)/shard_map/all_to_all | solution.py:23
  170.8 1.6 shard_map.84
  172.4 17.8 %all_to_all.50 = bf16[32,8,1024]{2,1,0:T(8,128)(2,1)S(1)} all-to-all(bf16[32,8,1024]{2,1,0:T(8,128)(2,1)S(1)} %shard_map.84), channel_id=1, replica_groups=mesh['y'=4,'x'=4,'zl'=8,'zh'=2,'c'=2] {'c','y','x'}, dimensions={0} | all-to-all | bytes 1048576 | tf_op jit(solution)/shard_map/all_to_all | solution.py:23
  190.3 0.6 fusion
  (26 shorter events, 0.2 us)
Async XLA Ops:
  0.0 20.1 %copy-start.13 = (bf16[1024]{0:T(1024)(128)(2,1)S(1)}, bf16[1024]{0:T(1024)(128)(2,1)}, u32[]{:S(2)}) copy-start(bf16[1024]{0:T(1024)(128)(2,1)} %param.11) | copy-start | bytes 6148
  0.8 12.9 %copy-start.8 = (s32[6]{0:T(128)}, s32[6]{0:T(128)S(1)}, u32[]{:S(2)}) copy-start(s32[6]{0:T(128)S(1)} %stack.24.place) | copy-start | bytes 76
  0.8 1.2 copy-start.4
  1.9 0.7 copy-start.12
  2.6 30.5 %copy-start.5 = (bf16[128,1024]{1,0:T(8,128)(2,1)S(1)}, bf16[128,1024]{1,0:T(8,128)(2,1)}, u32[]{:S(2)}) copy-start(bf16[128,1024]{1,0:T(8,128)(2,1)} %pool_ref.1) | copy-start | bytes 786436
  4.2 0.7 copy-start.6
  4.9 35.8 %collective-permute-start = (bf16[256,512]{1,0:T(8,128)(2,1)}, bf16[256,512]{1,0:T(8,128)(2,1)}, u32[]{:S(2)}, u32[]{:S(2)}) collective-permute-start(bf16[256,512]{1,0:T(8,128)(2,1)} %get-tuple-element.22), channel_id=1, source_target_pairs={{0,1},{1,0},{2,3},{3,2},{4,5},{5,4},{6,7},{7,6},{8,9},{9,8},{10,11... | collective-permute-start | bytes 786440 | tf_op jit(solution)/shard_map/ppermute | solution.py:371
  16.4 24.3 %copy-start.7 = (bf16[256,512]{1,0:T(8,128)(2,1)S(1)}, bf16[256,512]{1,0:T(8,128)(2,1)}, u32[]{:S(2)}) copy-start(bf16[256,512]{1,0:T(8,128)(2,1)} %copy-done.6) | copy-start | bytes 786436
  16.4 10.4 %all-to-all-start = ((bf16[16,16,128]{2,1,0:T(8,128)(2,1)}), bf16[16,16,128]{2,1,0:T(8,128)(2,1)S(1)}, u32[]{:S(2)}, u32[]{:S(2)}) async-start(bf16[16,16,128]{2,1,0:T(8,128)(2,1)} %shard_map.73), calls=%async_computation | async-start | bytes 131072 | tf_op jit(solution)/shard_map/all_to_all | solution.py:23
  26.8 0.7 copy-start.9
  27.5 13.3 %copy-start.11 = (s32[6]{0:T(128)S(1)}, s32[6]{0:T(128)}, u32[]{:S(2)}) copy-start(s32[6]{0:T(128)} %copy-done.8) | copy-start | bytes 76
  28.7 12.0 %all-to-all-start.1 = ((bf16[32,16,128]{2,1,0:T(8,128)(2,1)}), bf16[32,16,128]{2,1,0:T(8,128)(2,1)S(1)}, u32[]{:S(2)}, u32[]{:S(2)}) async-start(bf16[32,16,128]{2,1,0:T(8,128)(2,1)} %shard_map.74), calls=%async_computation.1 | async-start | bytes 262144 | tf_op jit(solution)/shard_map/all_to_all | solution.py:23
  33.2 1.5 copy-start
  34.7 0.7 copy-start.10
  40.7 56.6 %copy-start.2 = (bf16[896,1024]{1,0:T(8,128)(2,1)S(1)}, bf16[896,1024]{1,0:T(8,128)(2,1)}, u32[]{:S(2)}) copy-start(bf16[896,1024]{1,0:T(8,128)(2,1)} %down_hbm.3) | copy-start | bytes 5505028
  97.3 35.6 %copy-start.1 = (bf16[1024,896]{1,0:T(8,128)(2,1)S(1)}, bf16[1024,896]{1,0:T(8,128)(2,1)}, u32[]{:S(2)}) copy-start(bf16[1024,896]{1,0:T(8,128)(2,1)} %up_hbm.3) | copy-start | bytes 5505028
  119.9 13.0 %all-to-all-start.5 = ((bf16[32,8,512]{2,1,0:T(8,128)(2,1)}), bf16[32,8,512]{2,1,0:T(8,128)(2,1)S(1)}, u32[]{:S(2)}, u32[]{:S(2)}) async-start(bf16[32,8,512]{2,1,0:T(8,128)(2,1)} %shard_map.80), calls=%async_computation.5 | async-start | bytes 524288 | tf_op jit(solution)/shard_map/all_to_all | solution.py:23
  132.9 37.9 %copy-start.3 = (bf16[896,1024]{1,0:T(8,128)(2,1)S(1)}, bf16[896,1024]{1,0:T(8,128)(2,1)}, u32[]{:S(2)}) copy-start(bf16[896,1024]{1,0:T(8,128)(2,1)} %down_hbm.3) | copy-start | bytes 5505028
where the time goes:
time: 192 us; the launch traced here: 191 us
  blocking collectives  125 us (65%)
  starting transfers between devices  21.5 us (11%)
  Pallas kernels  19.8 us (10%)
  waiting for transfers between devices  18 us (9%)
  local copies, waits for them, and re-layouts  5.48 us (3%)
    all_to_all x6, blocking collectives, swap(): return lax.all_to_all(x, axis, split_axis=0, concat_axis=0, tiled=True)  125 us
    pallas_call x12, Pallas kernels, call(): pl.pallas_call(kernel, out_shape=tuple((jax.ShapeDtypeStruct(shape, BF) f...  19.8 us
    all_to_all x3, waiting for transfers between devices, swap(): return lax.all_to_all(x, axis, split_axis=0, concat_axis=0, tiled=True)  18 us
    all_to_all x3, starting transfers between devices, swap(): return lax.all_to_all(x, axis, split_axis=0, concat_axis=0, tiled=True)  12.7 us
    ppermute x1, starting transfers between devices, staged(): received = lax.ppermute(sent, 'c', [(0, 1), (1, 0)])  8.74 us
    unnamed x28, local copies, waits for them, and re-layouts  5.39 us
  transfers between devices with their start and end apart: 4, of which 3 were waited for; matrix products, arithmetic and copies ran while one was open for 0% of the time, Pallas kernels for 3%

commit v1 on v0

--- a/solution.py
+++ b/solution.py
@@ -68,7 +68,7 @@
 VMEM = pl.BlockSpec(memory_space=pltpu.VMEM)
 
 
-def call(kernel, shapes, place, *arrays, hbm=None, scratch=(), limit=16):
+def call(kernel, shapes, place, *arrays, hbm=None, scratch=()):
     specs = [pl.BlockSpec(memory_space=pltpu.SMEM)]
     if hbm is not None:
         arrays = (hbm, *arrays)
@@ -81,7 +81,7 @@
         in_specs=specs,
         out_specs=(VMEM,) * len(shapes),
         scratch_shapes=scratch,
-        compiler_params=pltpu.CompilerParams(vmem_limit_bytes=int(limit * 1024 * 1024)),
+        compiler_params=pltpu.CompilerParams(vmem_limit_bytes=16 * 1024 * 1024),
     )(place, *arrays)
 
 
@@ -111,8 +111,10 @@
     return jnp.where(place[0] == 0, x[:, :half], x[:, half:])
 
 
-def range_kernel(place, delta_hbm, part_ref, delta_ref, sem):
+def range_kernel(place, delta_hbm, tokens_ref, part_ref, kept_ref, sent_ref, delta_ref, sem):
+    core = place[0]
     rows, cols = delta_ref.shape
+    half = cols // 2
     split = rows // 2
     copies = [
         pltpu.make_async_copy(
@@ -139,17 +141,10 @@
         part_ref[i * parts : (i + 1) * parts] = (
             dot(delta, signs).astype(BF).reshape(parts, *part_ref.shape[1:])
         )
-
-
-def halves_kernel(place, delta_ref, tokens_ref, kept_ref, sent_ref):
-    core = place[0]
-    half = delta_ref.shape[1] // 2
-    delta = delta_ref[...].astype(BF)
-    left, right = delta[:, :half], delta[:, half:]
-    tokens = jnp.concatenate([column(tokens_ref[i : i + 1].astype(F32)) for i in range(2)], axis=0)
-    tokens = tokens[:, : RANK // 2].astype(BF)
-    kept_ref[...] = jnp.concatenate([jnp.where(core == 0, left, right), tokens], axis=1)
-    sent_ref[...] = jnp.concatenate([jnp.where(core == 0, right, left), tokens], axis=1)
+        left, right = delta[:, :half], delta[:, half:]
+        tokens = column(tokens_ref[i : i + 1].astype(F32))[:, : RANK // 2].astype(BF)
+        kept_ref[span] = jnp.concatenate([jnp.where(core == 0, left, right), tokens], axis=1)
+        sent_ref[span] = jnp.concatenate([jnp.where(core == 0, right, left), tokens], axis=1)
 
 
 def pick_kernel(place, kept_ref, got_ref, pick_ref):
@@ -357,16 +352,13 @@
         ]
     ).astype(jnp.int32)
     padded = half + RANK // 2
-    (part,) = call(
+    part, kept, sent = call(
         range_kernel,
-        ((16, rows // 16, RANK),),
+        ((16, rows // 16, RANK), (rows, padded), (rows, padded)),
         place,
+        token_rows[:, 0, :],
         hbm=weight_delta,
         scratch=(pltpu.VMEM((rows, cols), F32),),
-        limit=63.5,
-    )
-    kept, sent = call(
-        halves_kernel, ((rows, padded), (rows, padded)), place, weight_delta, token_rows[:, 0, :]
     )
     received = lax.ppermute(sent, "c", [(0, 1), (1, 0)])
     parts = swap(part, L)

time: 192 us -> 188 us (0.979)
  Pallas kernels: 19.8 us -> 17.1 us
    pallas_call x12 -> x11, Pallas kernels: 19.8 us -> 17.1 us  [call(): pl.pallas_call(kernel, out_shape=tuple((jax.ShapeDtypeStruct(shape, BF) f...]
    unnamed x28 -> x16, local copies, waits for them, and re-layouts: 5.39 us -> 4.32 us
  transfers between devices with their start and end apart: 4 -> 4, of which waited for: 3 -> 3; matrix products, arithmetic and copies ran while one was open for 0% -> 0% of each run, Pallas kernels for 3% -> 2%
where the time goes in v1:
time: 188 us; the launch traced here: 187 us
  blocking collectives  125 us (66%)
  starting transfers between devices  21.4 us (11%)
  waiting for transfers between devices  17.5 us (9%)
  Pallas kernels  17.1 us (9%)
  local copies, waits for them, and re-layouts  4.4 us (2%)
    all_to_all x6, blocking collectives, swap(): return lax.all_to_all(x, axis, split_axis=0, concat_axis=0, tiled=True)  125 us
    all_to_all x3, waiting for transfers between devices, swap(): return lax.all_to_all(x, axis, split_axis=0, concat_axis=0, tiled=True)  17.5 us
    pallas_call x11, Pallas kernels, call(): pl.pallas_call(kernel, out_shape=tuple((jax.ShapeDtypeStruct(shape, BF) f...  17.1 us
    all_to_all x3, starting transfers between devices, swap(): return lax.all_to_all(x, axis, split_axis=0, concat_axis=0, tiled=True)  12.6 us
    ppermute x1, starting transfers between devices, staged(): received = lax.ppermute(sent, 'c', [(0, 1), (1, 0)])  8.75 us
    unnamed x16, local copies, waits for them, and re-layouts  4.32 us
  transfers between devices with their start and end apart: 4, of which 3 were waited for; matrix products, arithmetic and copies ran while one was open for 0% of the time, Pallas kernels for 2%

profile of v1, /device:TPU:1, one launch (start us, length us, event | category | flops | bytes accessed | tf_op | source)
XLA Modules:
  0.0 187.2 jit_solution(10204682798025682508)
XLA Ops:
  0.7 0.1 stack.24.place
  0.7 1.2 copy-done.6
  1.9 0.7 copy-done.7
  2.6 2.6 %shard_map.73 = (bf16[16,16,128]{2,1,0:T(8,128)(2,1)}, bf16[256,512]{1,0:T(8,128)(2,1)S(1)}, bf16[256,512]{1,0:T(8,128)(2,1)S(1)}) custom-call(s32[6]{0:T(128)S(1)} %stack.24.place, f32[256,896]{1,0:T(8,128)S(1)} %copy-done.6, s32[2,128]{1,0:T(2,128)S(1)} %bitcast.11), custom_call_target="tpu_custom_call" | custom-call | tf_op jit(solution)/shard_map/pallas_call | solution.py:78
  5.2 8.7 %collective-permute-start = (bf16[256,512]{1,0:T(8,128)(2,1)S(1)}, bf16[256,512]{1,0:T(8,128)(2,1)S(1)}, u32[]{:S(2)}, u32[]{:S(2)}) collective-permute-start(bf16[256,512]{1,0:T(8,128)(2,1)S(1)} %get-tuple-element.24), channel_id=1, source_target_pairs={{0,1},{1,0},{2,3},{3,2},{4,5},{5,4},{6,7},{7,6},{8,9},{9,8},{10,11... | collective-permute-start | bytes 786440 | tf_op jit(solution)/shard_map/ppermute | solution.py:363
  13.9 3.5 %all-to-all-start = ((bf16[16,16,128]{2,1,0:T(8,128)(2,1)}), bf16[16,16,128]{2,1,0:T(8,128)(2,1)S(1)}, u32[]{:S(2)}, u32[]{:S(2)}) async-start(bf16[16,16,128]{2,1,0:T(8,128)(2,1)} %get-tuple-element.20), calls=%async_computation | async-start | bytes 131072 | tf_op jit(solution)/shard_map/all_to_all | solution.py:23
  17.5 0.7 broadcast_in_dim.12
  18.1 6.1 %all-to-all-done.parts_ref = bf16[16,16,128]{2,1,0:T(8,128)(2,1)S(1)} async-done(((bf16[16,16,128]{2,1,0:T(8,128)(2,1)}), bf16[16,16,128]{2,1,0:T(8,128)(2,1)S(1)}, u32[]{:S(2)}, u32[]{:S(2)}) %all-to-all-start) | async-done | bytes 65568 | tf_op jit(solution)/shard_map/all_to_all | solution.py:23
  24.2 1.2 shard_map.74
  25.4 4.5 %all-to-all-start.1 = ((bf16[32,16,128]{2,1,0:T(8,128)(2,1)}), bf16[32,16,128]{2,1,0:T(8,128)(2,1)S(1)}, u32[]{:S(2)}, u32[]{:S(2)}) async-start(bf16[32,16,128]{2,1,0:T(8,128)(2,1)} %shard_map.74), calls=%async_computation.1 | async-start | bytes 262144 | tf_op jit(solution)/shard_map/all_to_all | solution.py:23
  29.9 1.5 copy-done
  31.4 0.9 copy-done.4
  32.4 1.3 shard_map.75
  33.7 3.8 %all-to-all-done.1.basis_ref = bf16[32,16,128]{2,1,0:T(8,128)(2,1)S(1)} async-done(((bf16[32,16,128]{2,1,0:T(8,128)(2,1)}), bf16[32,16,128]{2,1,0:T(8,128)(2,1)S(1)}, u32[]{:S(2)}, u32[]{:S(2)}) %all-to-all-start.1) | async-done | bytes 131104 | tf_op jit(solution)/shard_map/all_to_all | solution.py:23
  37.5 0.9 shard_map.76
  38.3 30.7 %all_to_all.45.parts_ref = bf16[16,8,1152]{2,1,0:T(8,128)(2,1)S(1)} all-to-all(bf16[16,8,1152]{2,1,0:T(8,128)(2,1)S(1)} %shard_map.76), channel_id=1, replica_groups=mesh['y'=4,'x'=4,'zl'=8,'zh'=2,'c'=2] {'zl','zh'}, dimensions={0} | all-to-all | bytes 589824 | tf_op jit(solution)/shard_map/all_to_all | solution.py:23
  69.1 0.7 shard_map.77
  69.7 23.8 %all_to_all.46.z_ref = bf16[16,8,1152]{2,1,0:T(8,128)(2,1)S(1)} all-to-all(bf16[16,8,1152]{2,1,0:T(8,128)(2,1)S(1)} %shard_map.77), channel_id=1, replica_groups=mesh['y'=4,'x'=4,'zl'=8,'zh'=2,'c'=2] {'zl','zh'}, dimensions={0} | all-to-all | bytes 589824 | tf_op jit(solution)/shard_map/all_to_all | solution.py:23
  93.5 4.3 %shard_map.78 = (bf16[32,8,512]{2,1,0:T(8,128)(2,1)S(1)}, bf16[128,448]{1,0:T(8,128)(2,1)S(1)}, bf16[128,448]{1,0:T(8,128)(2,1)S(1)}) custom-call(s32[6]{0:T(128)S(1)} %stack.24.place, bf16[896,1024]{1,0:T(8,128)(2,1)S(1)} %copy-done.2, bf16[16,8,1152]{2,1,0:T(8,128)(2,1)S(1)} %all_to_all.46.z_ref), custom_call_target="tpu_custom_call" | custom-call | tf_op jit(solution)/shard_map/pallas_call | solution.py:78
  97.8 17.0 %all_to_all.47.parts_ref = bf16[32,8,512]{2,1,0:T(8,128)(2,1)S(1)} all-to-all(bf16[32,8,512]{2,1,0:T(8,128)(2,1)S(1)} %get-tuple-element.30), channel_id=1, replica_groups=mesh['y'=4,'x'=4,'zl'=8,'zh'=2,'c'=2] {'c','y','x'}, dimensions={0} | all-to-all | bytes 524288 | tf_op jit(solution)/shard_map/all_to_all | solution.py:23
  114.8 1.3 shard_map.79
  116.1 4.6 %all-to-all-start.5 = ((bf16[32,8,512]{2,1,0:T(8,128)(2,1)}), bf16[32,8,512]{2,1,0:T(8,128)(2,1)S(1)}, u32[]{:S(2)}, u32[]{:S(2)}) async-start(bf16[32,8,512]{2,1,0:T(8,128)(2,1)} %shard_map.79), calls=%async_computation.5 | async-start | bytes 524288 | tf_op jit(solution)/shard_map/all_to_all | solution.py:23
  120.7 0.7 shard_map.80.pick_ref
  121.4 7.7 %all-to-all-done.5.step_ref = bf16[32,8,512]{2,1,0:T(8,128)(2,1)S(1)} async-done(((bf16[32,8,512]{2,1,0:T(8,128)(2,1)}), bf16[32,8,512]{2,1,0:T(8,128)(2,1)S(1)}, u32[]{:S(2)}, u32[]{:S(2)}) %all-to-all-start.5) | async-done | bytes 262176 | tf_op jit(solution)/shard_map/all_to_all | solution.py:23
  129.1 2.0 %shard_map.81 = (bf16[16,8,512]{2,1,0:T(8,128)(2,1)S(1)}, bf16[8,1024]{1,0:T(8,128)(2,1)S(1)}) custom-call(s32[6]{0:T(128)S(1)} %stack.24.place, bf16[1024,896]{1,0:T(8,128)(2,1)S(1)} %copy-done.1, bf16[32,8,512]{2,1,0:T(8,128)(2,1)S(1)} %all-to-all-done.5.step_ref, bf16[128,1024]{1,0:T(8,128)(2,1)S(1)} %copy-done.5, f32[1,1024]{1,0:T(1,128)S(1)} %bitcast.10, ...), custom_call_target="tpu_custom_call" | custom-call | tf_op jit(solution)/shard_map/pallas_call | solution.py:78
  131.1 17.8 %all_to_all.48.parts_ref = bf16[16,8,512]{2,1,0:T(8,128)(2,1)S(1)} all-to-all(bf16[16,8,512]{2,1,0:T(8,128)(2,1)S(1)} %get-tuple-element.33), channel_id=1, replica_groups=mesh['y'=4,'x'=4,'zl'=8,'zh'=2,'c'=2] {'zl','zh'}, dimensions={0} | all-to-all | bytes 262144 | tf_op jit(solution)/shard_map/all_to_all | solution.py:23
  148.9 0.6 shard_map.82
  149.5 17.6 %all_to_all.49.z_ref = bf16[16,8,512]{2,1,0:T(8,128)(2,1)S(1)} all-to-all(bf16[16,8,512]{2,1,0:T(8,128)(2,1)S(1)} %shard_map.82), channel_id=1, replica_groups=mesh['y'=4,'x'=4,'zl'=8,'zh'=2,'c'=2] {'zl','zh'}, dimensions={0} | all-to-all | bytes 262144 | tf_op jit(solution)/shard_map/all_to_all | solution.py:23
  167.1 1.6 shard_map.83
  168.7 17.8 %all_to_all.50 = bf16[32,8,1024]{2,1,0:T(8,128)(2,1)S(1)} all-to-all(bf16[32,8,1024]{2,1,0:T(8,128)(2,1)S(1)} %shard_map.83), channel_id=1, replica_groups=mesh['y'=4,'x'=4,'zl'=8,'zh'=2,'c'=2] {'c','y','x'}, dimensions={0} | all-to-all | bytes 1048576 | tf_op jit(solution)/shard_map/all_to_all | solution.py:23
  186.5 0.1 convert_reduce_fusion
  186.6 0.6 fusion
  (13 shorter events, 0.0 us)
Async XLA Ops:
  0.7 1.2 copy-start.6
  1.9 0.7 copy-start.7
  5.2 32.3 %collective-permute-start = (bf16[256,512]{1,0:T(8,128)(2,1)S(1)}, bf16[256,512]{1,0:T(8,128)(2,1)S(1)}, u32[]{:S(2)}, u32[]{:S(2)}) collective-permute-start(bf16[256,512]{1,0:T(8,128)(2,1)S(1)} %get-tuple-element.24), channel_id=1, source_target_pairs={{0,1},{1,0},{2,3},{3,2},{4,5},{5,4},{6,7},{7,6},{8,9},{9,8},{10,11... | collective-permute-start | bytes 786440 | tf_op jit(solution)/shard_map/ppermute | solution.py:363
  13.9 10.3 %all-to-all-start = ((bf16[16,16,128]{2,1,0:T(8,128)(2,1)}), bf16[16,16,128]{2,1,0:T(8,128)(2,1)S(1)}, u32[]{:S(2)}, u32[]{:S(2)}) async-start(bf16[16,16,128]{2,1,0:T(8,128)(2,1)} %get-tuple-element.20), calls=%async_computation | async-start | bytes 131072 | tf_op jit(solution)/shard_map/all_to_all | solution.py:23
  25.4 12.0 %all-to-all-start.1 = ((bf16[32,16,128]{2,1,0:T(8,128)(2,1)}), bf16[32,16,128]{2,1,0:T(8,128)(2,1)S(1)}, u32[]{:S(2)}, u32[]{:S(2)}) async-start(bf16[32,16,128]{2,1,0:T(8,128)(2,1)} %shard_map.74), calls=%async_computation.1 | async-start | bytes 262144 | tf_op jit(solution)/shard_map/all_to_all | solution.py:23
  29.9 1.5 copy-start
  31.4 0.9 copy-start.4
  37.5 56.1 %copy-start.2 = (bf16[896,1024]{1,0:T(8,128)(2,1)S(1)}, bf16[896,1024]{1,0:T(8,128)(2,1)}, u32[]{:S(2)}) copy-start(bf16[896,1024]{1,0:T(8,128)(2,1)} %down_hbm.3) | copy-start | bytes 5505028
  93.5 35.6 %copy-start.1 = (bf16[1024,896]{1,0:T(8,128)(2,1)S(1)}, bf16[1024,896]{1,0:T(8,128)(2,1)}, u32[]{:S(2)}) copy-start(bf16[1024,896]{1,0:T(8,128)(2,1)} %up_hbm.3) | copy-start | bytes 5505028
  93.5 35.6 %copy-start.5 = (bf16[128,1024]{1,0:T(8,128)(2,1)S(1)}, bf16[128,1024]{1,0:T(8,128)(2,1)}, u32[]{:S(2)}) copy-start(bf16[128,1024]{1,0:T(8,128)(2,1)} %pool_ref.1) | copy-start | bytes 786436
  116.1 13.0 %all-to-all-start.5 = ((bf16[32,8,512]{2,1,0:T(8,128)(2,1)}), bf16[32,8,512]{2,1,0:T(8,128)(2,1)S(1)}, u32[]{:S(2)}, u32[]{:S(2)}) async-start(bf16[32,8,512]{2,1,0:T(8,128)(2,1)} %shard_map.79), calls=%async_computation.5 | async-start | bytes 524288 | tf_op jit(solution)/shard_map/all_to_all | solution.py:23
  129.1 38.0 %copy-start.3 = (bf16[896,1024]{1,0:T(8,128)(2,1)S(1)}, bf16[896,1024]{1,0:T(8,128)(2,1)}, u32[]{:S(2)}) copy-start(bf16[896,1024]{1,0:T(8,128)(2,1)} %down_hbm.3) | copy-start | bytes 5505028
